TPU v7x, 32 devices: a whole 2x2x4 slice. The times are simulated.
32 devices in a mesh: grp: 2 (over y), pen: 8 (over z, x), ch: 2 (over core).
Axes of the slice: x: 2, y: 2, z: 4, core: 2. Of those that a mesh axis runs over, the one named last changes fastest.
Arguments:
- features: bfloat16 [256, 32, 128, 256], P(('grp', 'pen'), 'ch'), parts along dimension 0, may hold values from -6 to 6
- spectral_weights: bfloat16 [1, 2, 16, 32, 32, 1024], P(None, None, None, None, 'ch', 'pen'), may hold values from -0.75 to 0.75
- bypass_weights: float32 [1, 32, 32], P(None, None, 'ch'), may hold values from -0.75 to 0.75
- bypass_bias: float32 [1, 32], P(None, 'ch'), may hold values from -1 to 1
Outputs:
- features_out: float32 [256, 32, 128, 256], P(('grp', 'pen'), 'ch'), parts along dimension 0
There are 2 independent parts, one for each index of `grp`. A program takes and returns all parts, laid end to end along the dimension named above; an argument that names none is the same for every part. Nothing has to cross between parts.
All inputs are finite; a program needn't handle non-finite values.
Results may differ from a plain program's by a relative error of at most 0.0003.
Values may be sent and summed in bfloat16 or wider, within the bound.
A program may use at most 192 MiB of HBM per device.

v0:
```python
import functools
import math

import jax
import jax.numpy as jnp
import ml_dtypes
import numpy as np
from jax import lax
from jax.experimental import pallas as pl
from jax.experimental.pallas import tpu as pltpu
from jax.sharding import PartitionSpec as P

HIGHEST = lax.Precision.HIGHEST
LANES = 128
MZ = 32
F32 = jnp.float32
BF16 = jnp.bfloat16


def tables(length, kept):
    offsets = np.arange(kept)
    freqs = np.where(offsets < kept // 2, offsets, length - kept + offsets)
    phases = (freqs[:, None] * np.arange(length)[None, :]) % length
    angles = phases.astype(np.float64) * (2.0 * math.pi / length)
    return np.cos(angles), np.sin(angles)


def split_np(table):
    table = table.astype(np.float32)
    high = table.astype(ml_dtypes.bfloat16)
    low = (table - high.astype(np.float32)).astype(ml_dtypes.bfloat16)
    return high, low


def split(value):
    high = value.astype(BF16)
    return high, (value - high.astype(F32)).astype(BF16)


def dot(left, right):
    return jnp.dot(left, right, preferred_element_type=F32)


def forward_kernel(x_ref, ty_ref, bh_ref, bl_ref, out_ref, y_ref, *, my, nsub):
    block, ch, _, nz = x_ref.shape
    parts = nz // LANES
    groups = my // nsub
    half = my * ch
    for b in range(block):
        for c in range(ch):
            both = dot(ty_ref[...], x_ref[b, c])
            rows = both[: 2 * my] + both[2 * my :]
            for part in range(parts):
                y_ref[b, part, pl.ds(c, 2 * my, stride=ch), :] = rows[
                    :, part * LANES : (part + 1) * LANES
                ]
    highs, lows = [], []
    for b in range(block):
        pieces = []
        for cs in range(2):
            loaded = [
                y_ref[b, part, cs * half : (cs + 1) * half, :].reshape(groups, nsub, ch, LANES)
                for part in range(parts)
            ]
            for sub in range(nsub):
                for part in range(parts):
                    pieces.append(loaded[part][:, sub].reshape(groups * ch, LANES))
        high, low = split(jnp.concatenate(pieces, axis=1))
        highs.append(high)
        lows.append(low)
    high = jnp.concatenate(highs, axis=0)
    low = jnp.concatenate(lows, axis=0)
    result = dot(high, bh_ref[...]) + dot(low, bh_ref[...]) + dot(high, bl_ref[...])
    result = result.reshape(block, groups, ch, 2 * LANES)
    for b in range(block):
        out_ref[:, b] = result[b]


def inverse_kernel(
    cx_ref, who_ref, g_ref, x_ref, mix_ref, bias_ref, zh_ref, zl_ref, ty_ref, out_ref, v_ref, w_ref
    , *, my, nsub, ysub
):
    step = pl.program_id(0)
    groups, mx, ch, _ = g_ref.shape
    _, all_ch, ny, nz = x_ref.shape
    parts = nz // LANES

    @pl.loop(0, groups)
    def _(group):
        real = jnp.zeros((ch, LANES), F32)
        imag = jnp.zeros((ch, LANES), F32)
        for j in range(mx):
            cos, sin = cx_ref[step, j], cx_ref[step, mx + j]
            g_re = g_ref[group, j, :, :LANES]
            g_im = g_ref[group, j, :, LANES:]
            real = real + (g_re * cos - g_im * sin)
            imag = imag + (g_im * cos + g_re * sin)
        v_ref[group, :, :LANES] = real
        v_ref[group, :, LANES:] = imag

    high, low = split(v_ref[...].reshape(groups * ch, 2 * LANES))
    for piece in range(nsub * 2):
        cols = slice(piece * nz, (piece + 1) * nz)
        waves = dot(high, zh_ref[:, cols]) + dot(low, zh_ref[:, cols]) + dot(high, zl_ref[:, cols])
        for part in range(parts):
            w_ref[piece, part] = waves[:, part * LANES : (part + 1) * LANES]
    for o in range(ch):
        rows = jnp.concatenate(
            [
                jnp.concatenate(
                    [w_ref[piece, part, pl.ds(o, groups, stride=ch), :] for part in range(parts)],
                    axis=1,
                )
                for piece in range(nsub * 2)
            ],
            axis=0,
        )
        high, low = split(rows)
        spectral = dot(ty_ref[...], jnp.concatenate([high, high, low], axis=0))
        out_ref[0, o] = spectral + bias_ref[0, o]
    first = who_ref[0]
    for at in range(0, ny, ysub):
        window = slice(at, at + ysub)
        cells = x_ref[0, :, window, :].reshape(all_ch * ysub, nz)
        bypass = dot(mix_ref[...], jnp.concatenate([cells, cells], axis=0))
        inner = bypass.reshape(ch, ysub, nz) + out_ref[0, :, window, :]
        own = x_ref[0, pl.ds(first, ch), window, :].astype(F32)
        cubic = inner * (1.0 + 0.044715 * (inner * inner))
        out_ref[0, :, window, :] = own + 0.5 * inner * (
            1.0 + jnp.tanh(math.sqrt(2.0 / math.pi) * cubic)
        )


def whole_vmem():
    return pl.BlockSpec(memory_space=pltpu.VMEM)


def forward_modes(features, my, mz):
    slabs, ch, ny, nz = features.shape
    nsub = LANES // mz
    groups = my // nsub
    cos_y, sin_y = tables(ny, my)
    cos_z, sin_z = tables(nz, mz)
    y_table = np.concatenate(split_np(np.concatenate([cos_y, sin_y]) * ny**-0.5), axis=0)
    pair = np.stack([np.stack([cos_z, -sin_z]), np.stack([-sin_z, -cos_z])]) * nz**-0.5
    z_table = np.einsum("crkz,st->cszrtk", pair, np.eye(nsub)).reshape(2 * nsub * nz, 2 * LANES)
    z_high, z_low = split_np(z_table)
    block = 2 if slabs % 2 == 0 else 1
    return pl.pallas_call(
        functools.partial(forward_kernel, my=my, nsub=nsub),
        grid=(slabs // block,),
        in_specs=[
            pl.BlockSpec((block, ch, ny, nz), lambda i: (i, 0, 0, 0)),
            whole_vmem(),
            whole_vmem(),
            whole_vmem(),
        ],
        out_specs=pl.BlockSpec((groups, block, ch, 2 * LANES), lambda i: (0, i, 0, 0)),
        out_shape=jax.ShapeDtypeStruct((groups, slabs, ch, 2 * LANES), F32),
        scratch_shapes=[pltpu.VMEM((block, nz // LANES, 2 * my * ch, LANES), F32)],
        compiler_params=pltpu.CompilerParams(vmem_limit_bytes=48 * 2**20),
        cost_estimate=pl.CostEstimate(
            flops=32 * slabs * ch * my * ny * nz, bytes_accessed=8 * features.size, transcendentals=0
        ),
        name="forward_modes",
    )(features, jnp.asarray(y_table), jnp.asarray(z_high), jnp.asarray(z_low))


def inverse_field(coefs, first, modes, gathered, mixing, bias, my, mz):
    slabs, all_ch, ny, nz = gathered.shape
    groups, mx, ch, _ = modes.shape
    nsub = LANES // mz
    ysub = 16
    cos_y, sin_y = tables(ny, my)
    cos_z, sin_z = tables(nz, mz)
    pair = np.stack([np.stack([cos_z, sin_z]), np.stack([-sin_z, cos_z])]) * mz**-0.5
    z_table = np.einsum("rckz,ts->rtkscz", pair, np.eye(nsub)).reshape(2 * LANES, 2 * nsub * nz)
    z_high, z_low = split_np(z_table)
    y_pair = np.stack([cos_y, -sin_y]).reshape(2, groups, nsub, ny) * my**-0.5
    y_high, y_low = split_np(y_pair.transpose(3, 2, 0, 1).reshape(ny, 2 * my))
    y_table = np.concatenate([y_high, y_low, y_high], axis=1)
    high = lax.reduce_precision(mixing, 8, 7)
    both = jnp.stack([high, mixing - high]).astype(BF16)
    eye = jnp.eye(ysub, dtype=BF16)
    mix = (
        both.transpose(2, 0, 1)[:, None, :, :, None] * eye[None, :, None, None, :]
    ).reshape(ch * ysub, 2 * all_ch * ysub)
    return pl.pallas_call(
        functools.partial(inverse_kernel, my=my, nsub=nsub, ysub=ysub),
        grid=(slabs,),
        in_specs=[
            pl.BlockSpec(memory_space=pltpu.SMEM),
            pl.BlockSpec(memory_space=pltpu.SMEM),
            whole_vmem(),
            pl.BlockSpec((1, all_ch, ny, nz), lambda i: (i, 0, 0, 0)),
            whole_vmem(),
            pl.BlockSpec(memory_space=pltpu.SMEM),
            whole_vmem(),
            whole_vmem(),
            whole_vmem(),
        ],
        out_specs=pl.BlockSpec((1, ch, ny, nz), lambda i: (i, 0, 0, 0)),
        out_shape=jax.ShapeDtypeStruct((slabs, ch, ny, nz), F32),
        scratch_shapes=[
            pltpu.VMEM((groups, ch, 2 * LANES), F32),
            pltpu.VMEM((2 * nsub, nz // LANES, groups * ch, LANES), F32),
        ],
        compiler_params=pltpu.CompilerParams(vmem_limit_bytes=60 * 2**20),
        name="inverse_field",
    )(
        coefs,
        first,
        modes,
        gathered,
        mix,
        bias,
        jnp.asarray(z_high),
        jnp.asarray(z_low),
        jnp.asarray(y_table),
    )


def local(features, spectral_weights, bypass_weights, bypass_bias, *, pens, kept):
    slabs, ch, ny, nz = features.shape
    _, _, mx, all_ch, _, owned = spectral_weights.shape
    nx = slabs * pens
    mz = MZ
    my = kept // mz
    groups = kept // LANES
    gathered = lax.all_gather(features, "ch", axis=1, tiled=True)
    modes = forward_modes(features, my, mz)
    if owned != LANES:
        modes = modes.reshape(groups, slabs, ch, 2, LANES).transpose(1, 2, 3, 0, 4)
        modes = modes.reshape(slabs, ch, 2, pens, owned).transpose(3, 0, 1, 2, 4)
        modes = modes.reshape(pens, slabs, ch, 2 * owned)
    modes = lax.all_to_all(modes, "pen", split_axis=0, concat_axis=0, tiled=True)
    modes = modes.reshape(nx, ch, 2 * owned)
    cos_x, sin_x = tables(nx, mx)
    forward_x = jnp.asarray((np.concatenate([cos_x, sin_x]) * nx**-0.5).astype(np.float32))
    waves = jnp.einsum("dx,xcl->dcl", forward_x, modes, precision=HIGHEST)
    real_x = waves[:mx, :, :owned] + waves[mx:, :, owned:]
    imag_x = waves[:mx, :, owned:] - waves[mx:, :, :owned]
    joined = lax.all_gather(
        jnp.concatenate([real_x, imag_x], axis=2), "ch", axis=1, tiled=True
    )
    real_x = joined[:, :, None, :owned]
    imag_x = joined[:, :, None, owned:]
    weight_re = spectral_weights[0, 0].astype(F32)
    weight_im = spectral_weights[0, 1].astype(F32)
    real_g = jnp.sum(real_x * weight_re - imag_x * weight_im, axis=1)
    imag_g = jnp.sum(imag_x * weight_re + real_x * weight_im, axis=1)
    mixed, gathered = lax.optimization_barrier(
        (jnp.concatenate([real_g, imag_g], axis=2), gathered)
    )
    mixed = lax.all_gather(mixed, "pen", axis=0)
    if owned != LANES:
        mixed = mixed.reshape(pens, mx, ch, 2, owned).transpose(1, 2, 3, 0, 4)
        mixed = mixed.reshape(mx, ch, 2, groups, LANES).transpose(3, 0, 1, 2, 4)
        mixed = mixed.reshape(groups, mx, ch, 2 * LANES)
    inverse_x = jnp.asarray((np.concatenate([cos_x, sin_x]) * mx**-0.5).T.astype(np.float32))
    coefs = lax.dynamic_slice_in_dim(inverse_x, lax.axis_index("pen") * slabs, slabs, 0)
    first = (lax.axis_index("ch") * ch).astype(jnp.int32).reshape(1)
    return inverse_field(
        coefs, first, mixed, gathered, bypass_weights[0], bypass_bias, my, mz
    )


def solution(mesh):
    pens = mesh.shape["pen"]

    def run(features, spectral_weights, bypass_weights, bypass_bias):
        body = functools.partial(local, pens=pens, kept=spectral_weights.shape[5])
        return jax.shard_map(
            body,
            mesh=mesh,
            in_specs=(
                P(("grp", "pen"), "ch", None, None),
                P(None, None, None, None, "ch", "pen"),
                P(None, None, "ch"),
                P(None, "ch"),
            ),
            out_specs=P(("grp", "pen"), "ch", None, None),
            check_vma=False,
        )(features, spectral_weights, bypass_weights, bypass_bias)

    return run
```

profile of v0, /device:TPU:0, one launch (start us, length us, event | category | flops | bytes accessed | tf_op | source)
XLA Modules:
  0.0 200.6 jit_solution(3055611697904365208)
XLA Ops:
  6.5 0.0 copy-start
  6.5 0.0 copy-start.1
  6.5 0.0 copy-start.2
  6.5 0.0 all-gather.4.cloned.1.call-start
  6.5 0.7 all-gather.4.cloned.1.call-update
  7.3 0.0 all-gather.6.cloned.1.call-start
  7.3 0.5 copy-done
  7.8 0.3 copy-done.1
  8.1 0.0 copy-done.2
  8.1 17.5 %forward_modes.1 = f32[8,16,16,256]{3,2,1,0:T(8,128)S(1)} custom-call(bf16[16,16,128,256]{3,2,1,0:T(8,128)(2,1)} %x_ref.1, bf16[128,128]{1,0:T(8,128)(2,1)S(1)} %copy-done.2, bf16[2048,256]{1,0:T(8,128)(2,1)S(1)} %copy-done.1, bf16[2048,256]{1,0:T(8,128)(2,1)S(1)} %copy-done), custom_call_target="tpu_custom_call" | custom-call | flops 8589934592 | bytes 67108864 | tf_op jit(solution)/shard_map/forward_modes/pallas_call | solution.py:149
  25.6 0.0 copy-start.4
  25.6 55.4 %all_to_all.5 = f32[8,16,16,256]{3,2,1,0:T(8,128)S(1)} all-to-all(f32[8,16,16,256]{3,2,1,0:T(8,128)S(1)} %forward_modes.1), channel_id=1, replica_groups=mesh['grp'=2,'pen'=8,'ch'=2] {'pen'}, dimensions={0} | all-to-all | bytes 4194304 | tf_op jit(solution)/shard_map/all_to_all | solution.py:236
  81.1 0.0 copy-start.3
  81.1 0.0 copy-done.4
  81.1 2.3 %fusion.4 = f32[32,16,256]{2,0,1:T(8,128)S(1)} fusion(f32[32,128,1]{1,0,2:T(8,128)S(1)} %copy-done.4, f32[128,16,256]{2,1,0:T(8,128)S(1)} %bitcast.17), kind=kOutput, calls=%fused_computation.8 | convolution fusion | flops 201326592 | bytes 2637824 | tf_op jit(solution)/shard_map/dx,xcl->dcl/dot_general | solution.py:240
  83.4 0.0 copy-start.5
  83.5 2.2 %all_gather.12 = f32[16,32,256]{2,0,1:T(8,128)S(1)} all-gather(f32[16,16,256]{2,0,1:T(8,128)S(1)} %pad_maximum_fusion), channel_id=1, replica_groups=mesh['grp'=2,'pen'=8,'ch'=2] {'ch'}, dimensions={1}, use_global_device_ids=true | all-gather | bytes 786432 | tf_op jit(solution)/shard_map/all_gather | solution.py:243
  85.7 0.1 copy.22
  85.8 0.1 copy.23
  85.9 0.0 copy-done.3
  85.9 1.4 fusion.1
  87.3 0.7 pad_maximum_fusion.1
  88.0 0.0 all-gather.4.cloned.1.call-done.x_ref
  88.0 0.0 all-gather.6.cloned.1.call-update
  88.1 0.0 copy-done.5
  88.1 2.4 %broadcast_multiply_fusion = bf16[16,16,2,32,16]{4,3,2,1,0:T(8,128)(2,1)} fusion(bf16[16,16]{1,0:T(8,128)(2,1)S(1)} %fusion.7, bf16[16,2,32]{2,1,0:T(2,128)(2,1)S(1)} %copy.24), kind=kLoop, calls=%fused_computation.10 | loop fusion | flops 262144 | bytes 526848 | tf_op jit(solution)/shard_map/mul | solution.py:186
  90.5 8.8 %mul.62.mix_ref = bf16[256,1024]{1,0:T(8,128)(2,1)} reshape(bf16[16,16,2,32,16]{4,3,2,1,0:T(8,128)(2,1)} %broadcast_multiply_fusion) | data formatting | bytes 1048576 | tf_op jit(solution)/shard_map/mul | solution.py:186
  99.3 1.3 constant_dynamic-slice_fusion.cx_ref
  100.6 35.7 %all-gather.6.cloned.1.call-done = f32[128,16,256]{2,1,0:T(8,128)} async-done(((f32[16,16,256]{2,1,0:T(8,128)}), f32[128,16,256]{2,1,0:T(8,128)}) %all-gather.6.cloned.1.call-update) | async-done | bytes 2097168 | tf_op jit(solution)/shard_map/all_gather | solution.py:255
  136.3 57.4 %inverse_field.1 = f32[16,16,128,256]{3,2,1,0:T(8,128)} custom-call(f32[16,32]{1,0:T(8,128)} %constant_dynamic-slice_fusion.cx_ref, s32[1]{0:T(128)} %bitcast.who_ref, f32[8,16,16,256]{3,2,1,0:T(8,128)} %bitcast.18, bf16[16,32,128,256]{3,2,1,0:T(8,128)(2,1)} %all-gather.4.cloned.1.call-done.x_ref, bf16[256,1024]{1,0:T(8,128)(2,1)} %mul.62.mix_ref, ...), custom_call_target="tpu_custom_call" | custom-call | tf_op jit(solution)/shard_map/inverse_field/pallas_call | solution.py:188
  (7 shorter events, 0.1 us)
Async XLA Ops:
  6.5 1.2 copy-start
  6.5 1.5 copy-start.1
  6.5 1.5 copy-start.2
  6.5 81.5 %all-gather.4.cloned.1.call-start = ((), (), s32[]{:S(2)}) async-start(), calls=%async_computation.1 | async-start | bytes 50331648 | tf_op jit(solution)/shard_map/all_gather | solution.py:230
  7.3 129.1 %all-gather.6.cloned.1.call-start = ((), (), s32[]{:S(2)}) async-start(), calls=%async_computation.2 | async-start | bytes 2359296 | tf_op jit(solution)/shard_map/all_gather | solution.py:255
  25.6 55.4 %copy-start.4 = (f32[32,128,1]{1,0,2:T(8,128)S(1)}, f32[32,128,1]{1,0,2:T(8,128)}, u32[]{:S(2)}) copy-start(f32[32,128,1]{1,0,2:T(8,128)} %constant.40) | copy-start | bytes 49156
  81.1 4.8 %copy-start.3 = (bf16[1,2,16,32,16,128]{5,4,3,2,1,0:T(8,128)(2,1)S(1)}, bf16[1,2,16,32,16,128]{5,4,3,2,1,0:T(8,128)(2,1)}, u32[]{:S(2)}) copy-start(bf16[1,2,16,32,16,128]{5,4,3,2,1,0:T(8,128)(2,1)} %param.13) | copy-start | bytes 12582916
  83.4 4.6 %copy-start.5 = (f32[1,32,16]{1,2,0:T(8,128)S(1)}, f32[1,32,16]{1,2,0:T(8,128)}, u32[]{:S(2)}) copy-start(f32[1,32,16]{1,2,0:T(8,128)} %param.14) | copy-start | bytes 6148
Sparse Core Ops, SparseCore 0:
  8.9 53.7 all-gather.3
  88.2 48.1 all-gather.5
where the time goes:
time: 201 us
  Pallas kernels  74.9 us (37%)
  blocking collectives  57.6 us (29%)
  waiting for transfers between devices  36.5 us (18%)
  between operations  13.5 us (7%)
  local copies, waits for them, and re-layouts  11.1 us (6%)
  other arithmetic  4.56 us (2%)
  matrix products  2.31 us (1%)
    pallas_call x1, Pallas kernels, inverse_field(): pl.pallas_call(functools.partial(inverse_kernel, my=my, nsub=nsub, ysub=y...  57.4 us
    all_to_all x1, blocking collectives, local(): lax.all_to_all(modes, 'pen', split_axis=0, concat_axis=0, tiled=True)  55.4 us
    all_gather x1, waiting for transfers between devices, local(): mixed = lax.all_gather(mixed, 'pen', axis=0)  35.7 us
    pallas_call x1, Pallas kernels, forward_modes(): pl.pallas_call(functools.partial(forward_kernel, my=my, nsub=nsub), grid=...  17.5 us
    mul x1, local copies, waits for them, and re-layouts, inverse_field(): both.transpose(2, 0, 1)[:, None, :, :, None] * eye[None, :, None, None, :]  8.83 us
  transfers between devices with their start and end apart: 2, of which 1 were waited for; matrix products, arithmetic and copies ran while one was open for 9% of the time, Pallas kernels for 9%

commit v1 on v0

v1 whole, which is shorter than its diff:
```python
import functools
import math

import jax
import jax.numpy as jnp
import ml_dtypes
import numpy as np
from jax import lax
from jax.experimental import pallas as pl
from jax.experimental.pallas import tpu as pltpu
from jax.sharding import PartitionSpec as P

HIGHEST = lax.Precision.HIGHEST
LANES = 128
MZ = 32
F32 = jnp.float32
BF16 = jnp.bfloat16


def tables(length, kept):
    offsets = np.arange(kept)
    freqs = np.where(offsets < kept // 2, offsets, length - kept + offsets)
    phases = (freqs[:, None] * np.arange(length)[None, :]) % length
    angles = phases.astype(np.float64) * (2.0 * math.pi / length)
    return np.cos(angles), np.sin(angles)


def split_np(table):
    table = table.astype(np.float32)
    high = table.astype(ml_dtypes.bfloat16)
    low = (table - high.astype(np.float32)).astype(ml_dtypes.bfloat16)
    return high, low


def split(value):
    high = value.astype(BF16)
    return high, (value - high.astype(F32)).astype(BF16)


def dot(left, right):
    return jnp.dot(left, right, preferred_element_type=F32)


def forward_kernel(x_ref, ty_ref, bh_ref, bl_ref, out_ref, y_ref, *, my, nsub):
    block, ch, _, nz = x_ref.shape
    parts = nz // LANES
    groups = my // nsub
    half = my * ch
    for b in range(block):
        for c in range(ch):
            both = dot(ty_ref[...], x_ref[b, c])
            rows = both[: 2 * my] + both[2 * my :]
            for part in range(parts):
                y_ref[b, part, pl.ds(c, 2 * my, stride=ch), :] = rows[
                    :, part * LANES : (part + 1) * LANES
                ]
    highs, lows = [], []
    for b in range(block):
        pieces = []
        for cs in range(2):
            loaded = [
                y_ref[b, part, cs * half : (cs + 1) * half, :].reshape(groups, nsub, ch, LANES)
                for part in range(parts)
            ]
            for sub in range(nsub):
                for part in range(parts):
                    pieces.append(loaded[part][:, sub].reshape(groups * ch, LANES))
        high, low = split(jnp.concatenate(pieces, axis=1))
        highs.append(high)
        lows.append(low)
    high = jnp.concatenate(highs, axis=0)
    low = jnp.concatenate(lows, axis=0)
    result = dot(high, bh_ref[...]) + dot(low, bh_ref[...]) + dot(high, bl_ref[...])
    result = result.reshape(block, groups, ch, 2 * LANES)
    for b in range(block):
        out_ref[:, b] = result[b]


MESH = pl.DeviceIdType.MESH
CHUNKS = 4


def odd_power(value, power):
    result, square = value, value * value
    while power > 1:
        result, power = result * square, power - 2
    return result


def encode(value, power, scale):
    return odd_power(value * scale, power).astype(WIRE)


def decode(code, power, scale):
    code = code.astype(F32)
    root = jnp.exp2(jnp.log2(jnp.abs(code)) * (1.0 / power)) * (1.0 / scale)
    return jnp.where(code < 0.0, -root, root)


WIRE = BF16
MODES_CODE = (7, 16.0)
MIXED_CODE = (5, 1.0)


def spectrum_kernel(
    x_ref, feat_ref, weight_ref, ty_ref, bh_ref, bl_ref, tx_ref, ix_ref, out_ref, field_ref,
    y_ref, send, recv, wide, fx, weight, partial, every, plain,
    send_sem, recv_sem, gsend_sem, grecv_sem, psend_sem, fsend_sem, frecv_sem, xsem, wsem,
    *, my, nsub, pens, near,
):
    step = pl.program_id(0)
    steps = pl.num_programs(0)
    me = lax.axis_index("pen")
    core = lax.axis_index("ch")
    block, ch, _, nz = x_ref.shape
    parts = nz // LANES
    groups = my // nsub
    half = my * ch
    mx = every.shape[1]
    slabs = recv.shape[1] * block
    far = pens // near
    nx = wide.shape[1] // ch
    nblocks = recv.shape[1]
    chunks = grecv_sem.shape[1]
    span = mx // chunks

    def field_copy(at):
        window = pl.ds(at * block, block)
        return pltpu.make_async_remote_copy(
            src_ref=feat_ref.at[window],
            dst_ref=field_ref.at[window],
            send_sem=fsend_sem.at[at],
            recv_sem=frecv_sem.at[at],
            device_id={"ch": 1 - core},
            device_id_type=MESH,
        )

    def modes_copy(at, shift, source):
        target = lax.rem(me + shift, pens)
        return pltpu.make_async_remote_copy(
            src_ref=send.at[at, target],
            dst_ref=recv.at[source, at],
            send_sem=send_sem.at[at, shift - 1],
            recv_sem=recv_sem.at[source, at],
            device_id={"pen": target},
            device_id_type=MESH,
        )

    def column_copy(chunk, shift, source):
        target = lax.rem(me + shift * near, pens)
        window = pl.ds(chunk * span, span)
        return pltpu.make_async_remote_copy(
            src_ref=every.at[me, window],
            dst_ref=every.at[source, window],
            send_sem=gsend_sem.at[chunk, shift - 1],
            recv_sem=grecv_sem.at[source, chunk],
            device_id={"pen": target},
            device_id_type=MESH,
        )

    def row_copy(chunk, shift, source, landing):
        base = me - lax.rem(me, near)
        target = base + lax.rem(me + shift, near)
        window = pl.ds(chunk * span, span)
        return pltpu.make_async_remote_copy(
            src_ref=every.at[source, window],
            dst_ref=every.at[landing, window],
            send_sem=psend_sem.at[source, chunk, shift - 1],
            recv_sem=grecv_sem.at[landing, chunk],
            device_id={"pen": target},
            device_id_type=MESH,
        )

    def weight_copy():
        return pltpu.make_async_copy(weight_ref.at[0], weight, wsem)

    def pair_copy():
        return pltpu.make_async_remote_copy(
            src_ref=fx.at[0],
            dst_ref=fx.at[1],
            send_sem=xsem.at[0],
            recv_sem=xsem.at[1],
            device_id={"ch": 1 - core},
            device_id_type=MESH,
        )

    @pl.when(step == 0)
    def _():
        barrier = pltpu.get_barrier_semaphore()
        for shift in range(1, pens):
            pl.semaphore_signal(
                barrier, inc=1, device_id={"pen": lax.rem(me + shift, pens)}, device_id_type=MESH
            )
        pl.semaphore_signal(barrier, inc=1, device_id={"ch": 1 - core}, device_id_type=MESH)
        pl.semaphore_wait(barrier, pens)
        for at in range(nblocks):
            field_copy(at).start()
        weight_copy().start()

    for b in range(block):
        for c in range(ch):
            both = dot(ty_ref[...], x_ref[b, c])
            rows = both[: 2 * my] + both[2 * my :]
            for part in range(parts):
                y_ref[b, part, pl.ds(c, 2 * my, stride=ch), :] = rows[
                    :, part * LANES : (part + 1) * LANES
                ]
    highs, lows = [], []
    for b in range(block):
        pieces = []
        for cs in range(2):
            loaded = [
                y_ref[b, part, cs * half : (cs + 1) * half, :].reshape(groups, nsub, ch, LANES)
                for part in range(parts)
            ]
            for sub in range(nsub):
                for part in range(parts):
                    pieces.append(loaded[part][:, sub].reshape(groups * ch, LANES))
        high, low = split(jnp.concatenate(pieces, axis=1))
        highs.append(high)
        lows.append(low)
    high = jnp.concatenate(highs, axis=0)
    low = jnp.concatenate(lows, axis=0)
    result = dot(high, bh_ref[...]) + dot(low, bh_ref[...]) + dot(high, bl_ref[...])
    result = encode(result, *MODES_CODE).reshape(block, groups, ch, 2 * LANES)
    for b in range(block):
        send[step, :, b] = result[b]
    recv[me, step] = send[step, me]
    for shift in range(1, pens):
        modes_copy(step, shift, me).start()

    @pl.when(step == steps - 1)
    def _():
        def widen(source, at):
            rows = decode(recv[source, at].reshape(block * ch, 2 * LANES), *MODES_CODE)
            window = pl.ds(pl.multiple_of((source * nblocks + at) * (block * ch), 8), block * ch)
            wide[0, window, :] = rows[:, :LANES]
            wide[1, window, :] = rows[:, LANES:]

        @pl.loop(0, nblocks)
        def _(at):
            widen(me, at)

        for shift in range(1, pens):
            source = lax.rem(me + pens - shift, pens)

            @pl.loop(0, nblocks)
            def _(at):
                modes_copy(at, shift, source).wait_recv()
                widen(source, at)

        for c in range(ch):
            rows = jnp.concatenate(
                [wide[part, pl.ds(c, nx, stride=ch), :] for part in range(2)], axis=1
            )
            high, low = split(rows)
            both = dot(tx_ref[...], jnp.concatenate([high, low], axis=0))
            waves = both[: 2 * mx] + both[2 * mx :]
            fx[0, 0, pl.ds(c, mx, stride=ch), :] = waves[:mx, :LANES] + waves[mx:, LANES:]
            fx[0, 1, pl.ds(c, mx, stride=ch), :] = waves[:mx, LANES:] - waves[mx:, :LANES]
        pair_copy().start()
        weight_copy().wait()

        def mix(slot, j, real, imag):
            first = (core if slot == 0 else 1 - core) * ch
            for c in range(ch):
                x_re = fx[slot, 0, pl.ds(j * ch + c, 1), :]
                x_im = fx[slot, 1, pl.ds(j * ch + c, 1), :]
                w_re = weight[0, j, first + c].astype(F32)
                w_im = weight[1, j, first + c].astype(F32)
                real = real + (x_re * w_re - x_im * w_im)
                imag = imag + (x_im * w_re + x_re * w_im)
            return real, imag

        @pl.loop(0, mx)
        def _(j):
            zero = jnp.zeros(partial.shape[2:], F32)
            partial[0, j], partial[1, j] = mix(0, j, zero, zero)

        pair_copy().wait()

        @pl.loop(0, chunks)
        def _(chunk):
            @pl.loop(0, span)
            def _(local_j):
                j = chunk * span + local_j
                real, imag = mix(1, j, partial[0, j], partial[1, j])
                coded = encode(jnp.concatenate([real, imag], axis=1), *MIXED_CODE)
                every[me, j] = coded

            for shift in range(1, far):
                column_copy(chunk, shift, me).start()
            for shift in range(1, near):
                row_copy(chunk, shift, me, me).start()

        @pl.loop(0, nblocks)
        def _(at):
            for shift in range(1, pens):
                modes_copy(at, shift, me).wait_send()

        @pl.loop(0, chunks)
        def _(chunk):
            for shift in range(1, far):
                source = lax.rem(me + pens - shift * near, pens)
                column_copy(chunk, shift, source).wait_recv()
                for side in range(1, near):
                    row_copy(chunk, side, source, source).start()

        def finish(source):
            @pl.loop(0, mx)
            def _(j):
                rows = decode(every[source, j], *MIXED_CODE)
                window = pl.ds(pl.multiple_of(j * ch, 8), ch)
                plain[0, window, :] = rows[:, :LANES]
                plain[1, window, :] = rows[:, LANES:]

            for o in range(ch):
                real = plain[0, pl.ds(o, mx, stride=ch), :]
                imag = plain[1, pl.ds(o, mx, stride=ch), :]
                rows = jnp.concatenate(
                    [
                        jnp.concatenate([real, imag], axis=1),
                        jnp.concatenate([imag, -real], axis=1),
                    ],
                    axis=0,
                )
                high, low = split(rows)
                waves = dot(ix_ref[...], jnp.concatenate([high, high, low], axis=0))
                window = pl.ds(o * groups + source, slabs, stride=groups * ch)
                out_ref[0, window, :] = waves[:, :LANES]
                out_ref[1, window, :] = waves[:, LANES:]

        @pl.loop(0, far)
        def _(shift):
            source = lax.rem(me + pens - shift * near, pens)
            finish(source)

        base = me - lax.rem(me, near)
        for side in range(1, near):
            @pl.loop(0, far)
            def _(shift):
                column = base + lax.rem(me + near - side, near)
                source = lax.rem(column + pens - shift * near, pens)

                @pl.loop(0, chunks)
                def _(chunk):
                    row_copy(chunk, side, source, source).wait_recv()

                finish(source)

        @pl.loop(0, chunks)
        def _(chunk):
            for shift in range(1, far):
                column_copy(chunk, shift, me).wait_send()
            for shift in range(far):
                source = lax.rem(me + pens - shift * near, pens)
                for side in range(1, near):
                    row_copy(chunk, side, source, source).wait_send()

        @pl.loop(0, nblocks)
        def _(at):
            field_copy(at).wait()


def forward_tables(ny, nz, my, mz):
    nsub = LANES // mz
    cos_y, sin_y = tables(ny, my)
    cos_z, sin_z = tables(nz, mz)
    y_table = np.concatenate(split_np(np.concatenate([cos_y, sin_y]) * ny**-0.5), axis=0)
    pair = np.stack([np.stack([cos_z, -sin_z]), np.stack([-sin_z, -cos_z])]) * nz**-0.5
    z_table = np.einsum("crkz,st->cszrtk", pair, np.eye(nsub)).reshape(2 * nsub * nz, 2 * LANES)
    return (y_table, *split_np(z_table))


def inverse_x_table(nx, mx):
    cos_x, sin_x = tables(nx, mx)
    high, low = split_np(np.concatenate([cos_x, -sin_x]).T * mx**-0.5)
    return np.concatenate([high, low, high], axis=1)


def spectrum(features, weights, my, mz, pens, near):
    slabs, ch, ny, nz = features.shape
    _, _, mx, all_ch, _, _ = weights.shape
    nx = slabs * pens
    nsub = LANES // mz
    groups = my // nsub
    y_table, z_high, z_low = forward_tables(ny, nz, my, mz)
    cos_x, sin_x = tables(nx, mx)
    x_high, x_low = split_np(np.concatenate([cos_x, sin_x]) * nx**-0.5)
    x_table = np.concatenate(
        [
            np.concatenate([x_high, x_high], axis=1),
            np.concatenate([x_low, np.zeros_like(x_low)], axis=1),
        ],
        axis=0,
    )
    inverse = lax.dynamic_slice_in_dim(
        jnp.asarray(inverse_x_table(nx, mx)), lax.axis_index("pen") * slabs, slabs, 0
    )
    block = 2 if slabs % 2 == 0 else 1
    nblocks = slabs // block
    chunks = CHUNKS if mx % CHUNKS == 0 else 1
    anywhere = pl.BlockSpec(memory_space=pl.ANY)
    return pl.pallas_call(
        functools.partial(spectrum_kernel, my=my, nsub=nsub, pens=pens, near=near),
        grid=(nblocks,),
        in_specs=[
            pl.BlockSpec((block, ch, ny, nz), lambda i: (i, 0, 0, 0)),
            anywhere,
            anywhere,
            whole_vmem(),
            whole_vmem(),
            whole_vmem(),
            whole_vmem(),
            whole_vmem(),
        ],
        out_specs=[whole_vmem(), anywhere],
        out_shape=[
            jax.ShapeDtypeStruct((2, slabs * ch * groups, LANES), F32),
            jax.ShapeDtypeStruct(features.shape, features.dtype),
        ],
        scratch_shapes=[
            pltpu.VMEM((block, nz // LANES, 2 * my * ch, LANES), F32),
            pltpu.VMEM((nblocks, pens, block, ch, 2 * LANES), WIRE),
            pltpu.VMEM((pens, nblocks, block, ch, 2 * LANES), WIRE),
            pltpu.VMEM((2, nx * ch, LANES), F32),
            pltpu.VMEM((2, 2, mx * ch, LANES), F32),
            pltpu.VMEM((2, mx, all_ch, ch, LANES), BF16),
            pltpu.VMEM((2, mx, ch, LANES), F32),
            pltpu.VMEM((pens, mx, ch, 2 * LANES), WIRE),
            pltpu.VMEM((2, mx * ch, LANES), F32),
            pltpu.SemaphoreType.DMA((nblocks, pens - 1)),
            pltpu.SemaphoreType.DMA((pens, nblocks)),
            pltpu.SemaphoreType.DMA((chunks, max(pens // near - 1, 1))),
            pltpu.SemaphoreType.DMA((pens, chunks)),
            pltpu.SemaphoreType.DMA((pens, chunks, max(near - 1, 1))),
            pltpu.SemaphoreType.DMA((nblocks,)),
            pltpu.SemaphoreType.DMA((nblocks,)),
            pltpu.SemaphoreType.DMA((2,)),
            pltpu.SemaphoreType.DMA,
        ],
        compiler_params=pltpu.CompilerParams(
            vmem_limit_bytes=60 * 2**20, collective_id=0, has_side_effects=True
        ),
        cost_estimate=pl.CostEstimate(
            flops=32 * slabs * ch * my * ny * nz, bytes_accessed=8 * features.size, transcendentals=0
        ),
        name="spectrum",
    )(
        features,
        features,
        weights,
        jnp.asarray(y_table),
        jnp.asarray(z_high),
        jnp.asarray(z_low),
        jnp.asarray(x_table),
        inverse,
    )


def inverse_kernel(
    h_ref, x_ref, peer_ref, mix_ref, rows_ref, cols_ref, mask_ref, bias_ref, ty_ref, tz_ref, out_ref,
    table,
    *, nsub, groups, ysub
):
    _, ch, ny, nz = x_ref.shape

    @pl.when(pl.program_id(0) == 0)
    def _():
        for at, part in enumerate(split(mix_ref[...])):
            wide = dot(dot(rows_ref[...], part).astype(BF16), cols_ref[...]) * mask_ref[...]
            table[pl.ds(at * ch * ysub, ch * ysub), :] = wide.astype(BF16)

    count = LANES // MZ
    block = lax.broadcasted_iota(jnp.int32, (ch * groups, LANES), 1) // MZ
    real, imag = h_ref[0], h_ref[1]

    def rolled(rows):
        return [rows] + [pltpu.roll(rows, MZ * at, 1) for at in range(1, count)]

    reals, imags = rolled(real), rolled(imag)
    minus = [-rows for rows in reals]

    def laid(even, odd, sub):
        result = even[-sub % count]
        for at in range(1, count):
            result = jnp.where(block == at, (odd if at % 2 else even)[(at - sub) % count], result)
        return result

    tops = [laid(reals, imags, sub) for sub in range(nsub)]
    lows = [laid(imags, minus, sub) for sub in range(nsub)]
    for pair in range(0, ch, 2):
        sides = []
        for o in (pair, pair + 1):
            window = slice(o * groups, (o + 1) * groups)
            high, low = split(jnp.concatenate([rows[window] for rows in tops + lows], axis=0))
            sides.append(jnp.concatenate([high, high, low], axis=0))
        waves = dot(ty_ref[...], jnp.concatenate(sides, axis=1))
        for at, o in enumerate((pair, pair + 1)):
            high, low = split(waves[:, at * LANES : (at + 1) * LANES])
            spectral = dot(jnp.concatenate([high, low], axis=1), tz_ref[...])
            out_ref[0, o] = spectral + bias_ref[0, o]
    for at in range(0, ny, ysub):
        window = slice(at, at + ysub)
        cells = [ref[0, c, window, :] for ref in (x_ref, peer_ref) for c in range(ch)]
        both = dot(table[...], jnp.concatenate(cells, axis=0))
        bypass = both[: ch * ysub] + both[ch * ysub :]
        inner = bypass.reshape(ch, ysub, nz) + out_ref[0, :, window, :]
        own = x_ref[0, :, window, :].astype(F32)
        scale = math.sqrt(2.0 / math.pi)
        cubic = inner * (scale + (0.044715 * scale) * (inner * inner))
        half = 0.5 * inner
        out_ref[0, :, window, :] = own + (half + half * jnp.tanh(cubic))


def whole_vmem():
    return pl.BlockSpec(memory_space=pltpu.VMEM)


def forward_modes(features, my, mz):
    slabs, ch, ny, nz = features.shape
    nsub = LANES // mz
    groups = my // nsub
    cos_y, sin_y = tables(ny, my)
    cos_z, sin_z = tables(nz, mz)
    y_table = np.concatenate(split_np(np.concatenate([cos_y, sin_y]) * ny**-0.5), axis=0)
    pair = np.stack([np.stack([cos_z, -sin_z]), np.stack([-sin_z, -cos_z])]) * nz**-0.5
    z_table = np.einsum("crkz,st->cszrtk", pair, np.eye(nsub)).reshape(2 * nsub * nz, 2 * LANES)
    z_high, z_low = split_np(z_table)
    block = 2 if slabs % 2 == 0 else 1
    return pl.pallas_call(
        functools.partial(forward_kernel, my=my, nsub=nsub),
        grid=(slabs // block,),
        in_specs=[
            pl.BlockSpec((block, ch, ny, nz), lambda i: (i, 0, 0, 0)),
            whole_vmem(),
            whole_vmem(),
            whole_vmem(),
        ],
        out_specs=pl.BlockSpec((groups, block, ch, 2 * LANES), lambda i: (0, i, 0, 0)),
        out_shape=jax.ShapeDtypeStruct((groups, slabs, ch, 2 * LANES), F32),
        scratch_shapes=[pltpu.VMEM((block, nz // LANES, 2 * my * ch, LANES), F32)],
        compiler_params=pltpu.CompilerParams(vmem_limit_bytes=48 * 2**20),
        cost_estimate=pl.CostEstimate(
            flops=32 * slabs * ch * my * ny * nz, bytes_accessed=8 * features.size, transcendentals=0
        ),
        name="forward_modes",
    )(features, jnp.asarray(y_table), jnp.asarray(z_high), jnp.asarray(z_low))


def inverse_field(waves, features, peer, mixing, bias, my, mz):
    slabs, ch, ny, nz = features.shape
    all_ch = mixing.shape[0]
    nsub = LANES // mz
    groups = my // nsub
    ysub = YSUB
    cos_y, sin_y = tables(ny, my)
    cos_z, sin_z = tables(nz, mz)
    y_pair = np.stack([cos_y, -sin_y]).reshape(2, groups, nsub, ny) * my**-0.5
    y_high, y_low = split_np(y_pair.transpose(3, 0, 2, 1).reshape(ny, 2 * my))
    y_table = np.concatenate([y_high, y_low, y_high], axis=1)
    z_high, z_low = split_np(np.concatenate([cos_z, -sin_z]) * mz**-0.5)
    copies = LANES // (2 * mz)
    blank = [np.zeros_like(z_high)] * (copies - 2)
    z_table = np.concatenate(
        [z_high, z_low, *blank, z_high, np.zeros_like(z_high), *blank], axis=0
    )
    high_rows, high_cols = ch * ysub, all_ch * ysub
    spread_rows = np.repeat(np.eye(ch), ysub, axis=0).astype(ml_dtypes.bfloat16)
    spread_cols = np.repeat(np.eye(all_ch), ysub, axis=1).astype(ml_dtypes.bfloat16)
    mask = np.tile(np.eye(ysub), (ch, all_ch)).astype(np.float32)
    rows = ch * groups
    return pl.pallas_call(
        functools.partial(inverse_kernel, nsub=nsub, groups=groups, ysub=ysub),
        grid=(slabs,),
        in_specs=[
            pl.BlockSpec((2, rows, LANES), lambda i: (0, i, 0)),
            pl.BlockSpec((1, ch, ny, nz), lambda i: (i, 0, 0, 0)),
            pl.BlockSpec((1, ch, ny, nz), lambda i: (i, 0, 0, 0)),
            whole_vmem(),
            whole_vmem(),
            whole_vmem(),
            whole_vmem(),
            pl.BlockSpec(memory_space=pltpu.SMEM),
            whole_vmem(),
            whole_vmem(),
        ],
        out_specs=pl.BlockSpec((1, ch, ny, nz), lambda i: (i, 0, 0, 0)),
        out_shape=jax.ShapeDtypeStruct((slabs, ch, ny, nz), F32),
        scratch_shapes=[pltpu.VMEM((2 * high_rows, high_cols), BF16)],
        compiler_params=pltpu.CompilerParams(vmem_limit_bytes=60 * 2**20),
        name="inverse_field",
    )(
        waves,
        features,
        peer,
        mixing.T,
        jnp.asarray(spread_rows),
        jnp.asarray(spread_cols),
        jnp.asarray(mask),
        bias,
        jnp.asarray(y_table),
        jnp.asarray(z_table),
    )


YSUB = 8


def spread_spectrum(features, spectral_weights, my, mz, pens):
    slabs, ch, _, _ = features.shape
    _, _, mx, _, _, owned = spectral_weights.shape
    nx = slabs * pens
    groups = my * mz // LANES
    modes = forward_modes(features, my, mz)
    modes = modes.reshape(groups, slabs, ch, 2, LANES).transpose(1, 2, 3, 0, 4)
    modes = modes.reshape(slabs, ch, 2, pens, owned).transpose(3, 0, 1, 2, 4)
    modes = modes.reshape(pens, slabs, ch, 2 * owned)
    modes = lax.all_to_all(modes, "pen", split_axis=0, concat_axis=0, tiled=True)
    modes = modes.reshape(nx, ch, 2 * owned)
    cos_x, sin_x = tables(nx, mx)
    forward_x = jnp.asarray((np.concatenate([cos_x, sin_x]) * nx**-0.5).astype(np.float32))
    waves = jnp.einsum("dx,xcl->dcl", forward_x, modes, precision=HIGHEST)
    real_x = waves[:mx, :, :owned] + waves[mx:, :, owned:]
    imag_x = waves[:mx, :, owned:] - waves[mx:, :, :owned]
    joined = lax.all_gather(
        jnp.concatenate([real_x, imag_x], axis=2), "ch", axis=1, tiled=True
    )
    real_x = joined[:, :, None, :owned]
    imag_x = joined[:, :, None, owned:]
    weight_re = spectral_weights[0, 0].astype(F32)
    weight_im = spectral_weights[0, 1].astype(F32)
    real_g = jnp.sum(real_x * weight_re - imag_x * weight_im, axis=1)
    imag_g = jnp.sum(imag_x * weight_re + real_x * weight_im, axis=1)
    mixed = lax.all_gather(jnp.concatenate([real_g, imag_g], axis=2), "pen", axis=0)
    mixed = mixed.reshape(pens, mx, ch, 2, owned).transpose(1, 2, 3, 0, 4)
    mixed = mixed.reshape(mx, ch, 2, groups, LANES).transpose(3, 0, 1, 2, 4)
    mixed = mixed.reshape(groups, mx, ch, 2, LANES)
    table = inverse_x_table(nx, mx)[:, : 2 * mx].astype(np.float32)
    table = table + inverse_x_table(nx, mx)[:, 2 * mx : 4 * mx].astype(np.float32)
    table = lax.dynamic_slice_in_dim(
        jnp.asarray(table), lax.axis_index("pen") * slabs, slabs, 0
    )
    real, imag = mixed[:, :, :, 0], mixed[:, :, :, 1]
    pair = jnp.stack([jnp.concatenate([real, imag], 1), jnp.concatenate([imag, -real], 1)])
    waves = jnp.einsum("xj,pgjol->pxogl", table, pair, precision=HIGHEST)
    return waves.reshape(2, slabs * ch * groups, LANES)


def local(features, spectral_weights, bypass_weights, bypass_bias, *, pens, kept):
    slabs, ch, _, _ = features.shape
    _, _, mx, all_ch, _, owned = spectral_weights.shape
    mz = MZ
    my = kept // mz
    near = 2 if pens % 2 == 0 else 1
    core = lax.axis_index("ch")
    if owned == LANES and all_ch == 2 * ch:
        waves, peer = spectrum(features, spectral_weights, my, mz, pens, near)
    else:
        peer = lax.ppermute(features, "ch", [(0, 1), (1, 0)])
        waves = spread_spectrum(features, spectral_weights, my, mz, pens)
    mixing = bypass_weights[0]
    mixing = jnp.where(core == 0, mixing, jnp.roll(mixing, ch, axis=0))
    return inverse_field(waves, features, peer, mixing, bypass_bias, my, mz)


def solution(mesh):
    pens = mesh.shape["pen"]

    def run(features, spectral_weights, bypass_weights, bypass_bias):
        body = functools.partial(local, pens=pens, kept=spectral_weights.shape[5])
        return jax.shard_map(
            body,
            mesh=mesh,
            in_specs=(
                P(("grp", "pen"), "ch", None, None),
                P(None, None, None, None, "ch", "pen"),
                P(None, None, "ch"),
                P(None, "ch"),
            ),
            out_specs=P(("grp", "pen"), "ch", None, None),
            check_vma=False,
        )(features, spectral_weights, bypass_weights, bypass_bias)

    return run
```

time: 201 us -> 110 us (0.55)
  blocking collectives: 57.6 us -> 0 us
  waiting for transfers between devices: 36.5 us -> 0 us
  Pallas kernels: 74.9 us -> 106 us
  between operations: 13.5 us -> 0.01 us
  local copies, waits for them, and re-layouts: 11.1 us -> 2.12 us
  other arithmetic: 4.56 us -> 1.37 us
  matrix products: 2.31 us -> 0 us
    all_to_all x1 -> x0, blocking collectives: 55.4 us -> none  [local(): lax.all_to_all(modes, 'pen', split_axis=0, concat_axis=0, tiled=True)]
    all_gather x2 -> x0, waiting for transfers between devices: 35.7 us -> none  [the longest x1 35.7 us: local(): mixed = lax.all_gather(mixed, 'pen', axis=0)]
    pallas_call x2, Pallas kernels: 74.9 us -> 106 us  [the longest x1 59.4 us: spectrum(): pl.pallas_call(functools.partial(spectrum_kernel, my=my, nsub=nsub, pens=...]
    mul x1 -> x0, local copies, waits for them, and re-layouts: 8.83 us -> none  [inverse_field(): both.transpose(2, 0, 1)[:, None, :, :, None] * eye[None, :, None, None, :]]
    mul x1 -> x0, other arithmetic: 2.36 us -> none  [inverse_field(): both.transpose(2, 0, 1)[:, None, :, :, None] * eye[None, :, None, None, :]]
    dot_general x1 -> x0, matrix products: 2.31 us -> none  [local(): waves = jnp.einsum('dx,xcl->dcl', forward_x, modes, precision=HIGHEST)]
    all_gather x1 -> x0, blocking collectives: 2.18 us -> none  [local(): lax.all_gather(jnp.concatenate([real_x, imag_x], axis=2), 'ch', axis=1, t...]
  transfers between devices with their start and end apart: 2 -> 0, of which waited for: 1 -> 0; matrix products, arithmetic and copies ran while one was open for 9% -> 0% of each run, Pallas kernels for 9% -> 0%
where the time goes in v1:
time: 110 us
  Pallas kernels  106 us (96%)
  local copies, waits for them, and re-layouts  2.12 us (2%)
  other arithmetic  1.37 us (1%)
    pallas_call x1, Pallas kernels, spectrum(): pl.pallas_call(functools.partial(spectrum_kernel, my=my, nsub=nsub, pens=...  59.4 us
    pallas_call x1, Pallas kernels, inverse_field(): pl.pallas_call(functools.partial(inverse_kernel, nsub=nsub, groups=groups...  46.9 us

profile of v1, /device:TPU:0, one launch (start us, length us, event | category | flops | bytes accessed | tf_op | source)
XLA Modules:
  0.0 109.8 jit_solution(6453262854764358337)
XLA Ops:
  0.0 1.3 %constant_dynamic-slice_fusion.ix_ref = bf16[16,96]{1,0:T(8,128)(2,1)} fusion(bf16[128,96]{1,0:T(8,128)(2,1)} %constant.34.clone, s32[]{:T(128)S(6)} %select_n.11), kind=kLoop, calls=%fused_computation.4 | loop fusion | bytes 6148 | tf_op jit(solution)/shard_map/dynamic_slice | solution.py:397
  1.3 0.8 slice_bitcast_fusion.1
  2.1 1.4 %fusion.mix_ref = f32[16,32]{1,0:T(8,128)} fusion(f32[16,16]{0,1:T(8,128)S(1)} %get-tuple-element.10, f32[16,16]{0,1:T(8,128)S(1)} %get-tuple-element.9, f32[1,32,16]{1,2,0:T(8,128)} %param.16, pred[]{:T(512)S(6)} %eq.3), kind=kLoop, calls=%fused_computation.1 | loop fusion | flops 1024 | bytes 6145 | tf_op jit(solution)/shard_map/transpose | solution.py:597
  3.5 59.4 %spectrum.1 = (f32[2,2048,128]{2,1,0:T(8,128)}, bf16[16,16,128,256]{3,2,1,0:T(8,128)(2,1)}) custom-call(bf16[16,16,128,256]{3,2,1,0:T(8,128)(2,1)} %x_ref.3, bf16[16,16,128,256]{3,2,1,0:T(8,128)(2,1)} %x_ref.3, bf16[1,2,16,32,16,128]{5,4,3,2,1,0:T(8,128)(2,1)} %weight_ref.1, bf16[128,128]{1,0:T(8,128)(2,1)} %constant.35.clone.ty_ref, ...), custom_call_target="tpu_custom_call" | custom-call | flops 8589934592 | bytes 67108864 | tf_op jit(solution)/shard_map/spectrum/pallas_call | solution.py:404
  62.9 46.9 %inverse_field.1 = f32[16,16,128,256]{3,2,1,0:T(8,128)} custom-call(f32[2,2048,128]{2,1,0:T(8,128)} %get-tuple-element.7.h_ref, bf16[16,16,128,256]{3,2,1,0:T(8,128)(2,1)} %x_ref.3, bf16[16,16,128,256]{3,2,1,0:T(8,128)(2,1)} %get-tuple-element.8.peer_ref, f32[16,32]{1,0:T(8,128)} %fusion.mix_ref, bf16[128,16]{1,0:T(8,128)(2,1)} %constant.39.clone.rows_ref, ...), custom_call_target="tpu_custom_call" | custom-call | tf_op jit(solution)/shard_map/inverse_field/pallas_call | solution.py:573

commit v2 on v1

--- a/solution.py
+++ b/solution.py
@@ -78,6 +78,7 @@
 
 MESH = pl.DeviceIdType.MESH
 CHUNKS = 4
+TOGETHER = 2
 
 
 def odd_power(value, power):
@@ -98,15 +99,20 @@
 
 
 WIRE = BF16
-MODES_CODE = (7, 16.0)
-MIXED_CODE = (5, 1.0)
+FIELD_MAX = 6.0
+WEIGHT_MAX = 0.75
+
+
+def code_of(power, bound):
+    reach = 2.0 ** (126.0 / power)
+    return power, 2.0 ** math.floor(math.log2(reach / bound))
 
 
 def spectrum_kernel(
     x_ref, feat_ref, weight_ref, ty_ref, bh_ref, bl_ref, tx_ref, ix_ref, out_ref, field_ref,
     y_ref, send, recv, wide, fx, weight, partial, every, plain,
     send_sem, recv_sem, gsend_sem, grecv_sem, psend_sem, fsend_sem, frecv_sem, xsem, wsem,
-    *, my, nsub, pens, near,
+    *, my, nsub, pens, near, modes_code, mixed_code,
 ):
     step = pl.program_id(0)
     steps = pl.num_programs(0)
@@ -117,15 +123,17 @@
     groups = my // nsub
     half = my * ch
     mx = every.shape[1]
-    slabs = recv.shape[1] * block
     far = pens // near
     nx = wide.shape[1] // ch
-    nblocks = recv.shape[1]
+    nblocks = recv.shape[0]
+    bunch = recv.shape[2]
+    together = bunch // block
+    slabs = nblocks * bunch
     chunks = grecv_sem.shape[1]
     span = mx // chunks
 
     def field_copy(at):
-        window = pl.ds(at * block, block)
+        window = pl.ds(at * bunch, bunch)
         return pltpu.make_async_remote_copy(
             src_ref=feat_ref.at[window],
             dst_ref=field_ref.at[window],
@@ -139,7 +147,7 @@
         target = lax.rem(me + shift, pens)
         return pltpu.make_async_remote_copy(
             src_ref=send.at[at, target],
-            dst_ref=recv.at[source, at],
+            dst_ref=recv.at[at, source],
             send_sem=send_sem.at[at, shift - 1],
             recv_sem=recv_sem.at[source, at],
             device_id={"pen": target},
@@ -222,32 +230,29 @@
     high = jnp.concatenate(highs, axis=0)
     low = jnp.concatenate(lows, axis=0)
     result = dot(high, bh_ref[...]) + dot(low, bh_ref[...]) + dot(high, bl_ref[...])
-    result = encode(result, *MODES_CODE).reshape(block, groups, ch, 2 * LANES)
+    result = encode(result, *modes_code).reshape(block, groups, ch, 2 * LANES)
+    group, turn = step // together, step % together
     for b in range(block):
-        send[step, :, b] = result[b]
-    recv[me, step] = send[step, me]
-    for shift in range(1, pens):
-        modes_copy(step, shift, me).start()
+        send[group, :, turn * block + b] = result[b]
+
+    @pl.when(turn == together - 1)
+    def _():
+        recv[group, me] = send[group, me]
+        for away in range(1, pens):
+            shift = pens // 2 + (away // 2 if away % 2 else -(away // 2))
+            modes_copy(group, shift, me).start()
 
     @pl.when(step == steps - 1)
     def _():
-        def widen(source, at):
-            rows = decode(recv[source, at].reshape(block * ch, 2 * LANES), *MODES_CODE)
-            window = pl.ds(pl.multiple_of((source * nblocks + at) * (block * ch), 8), block * ch)
-            wide[0, window, :] = rows[:, :LANES]
-            wide[1, window, :] = rows[:, LANES:]
-
         @pl.loop(0, nblocks)
         def _(at):
-            widen(me, at)
-
-        for shift in range(1, pens):
-            source = lax.rem(me + pens - shift, pens)
-
-            @pl.loop(0, nblocks)
-            def _(at):
-                modes_copy(at, shift, source).wait_recv()
-                widen(source, at)
+            for shift in range(1, pens):
+                modes_copy(at, shift, lax.rem(me + pens - shift, pens)).wait_recv()
+            rows = decode(recv[at].reshape(pens, bunch * ch, 2 * LANES), *modes_code)
+            for source in range(pens):
+                start = pl.multiple_of((source * nblocks + at) * (bunch * ch), 8)
+                wide[0, pl.ds(start, bunch * ch), :] = rows[source, :, :LANES]
+                wide[1, pl.ds(start, bunch * ch), :] = rows[source, :, LANES:]
 
         for c in range(ch):
             rows = jnp.concatenate(
@@ -285,7 +290,7 @@
             def _(local_j):
                 j = chunk * span + local_j
                 real, imag = mix(1, j, partial[0, j], partial[1, j])
-                coded = encode(jnp.concatenate([real, imag], axis=1), *MIXED_CODE)
+                coded = encode(jnp.concatenate([real, imag], axis=1), *mixed_code)
                 every[me, j] = coded
 
             for shift in range(1, far):
@@ -298,21 +303,12 @@
             for shift in range(1, pens):
                 modes_copy(at, shift, me).wait_send()
 
-        @pl.loop(0, chunks)
-        def _(chunk):
-            for shift in range(1, far):
-                source = lax.rem(me + pens - shift * near, pens)
-                column_copy(chunk, shift, source).wait_recv()
-                for side in range(1, near):
-                    row_copy(chunk, side, source, source).start()
+        x_back = ix_ref[pl.ds(pl.multiple_of(me * slabs, 8), slabs), :]
 
         def finish(source):
-            @pl.loop(0, mx)
-            def _(j):
-                rows = decode(every[source, j], *MIXED_CODE)
-                window = pl.ds(pl.multiple_of(j * ch, 8), ch)
-                plain[0, window, :] = rows[:, :LANES]
-                plain[1, window, :] = rows[:, LANES:]
+            rows = decode(every[source].reshape(mx * ch, 2 * LANES), *mixed_code)
+            plain[0] = rows[:, :LANES]
+            plain[1] = rows[:, LANES:]
 
             for o in range(ch):
                 real = plain[0, pl.ds(o, mx, stride=ch), :]
@@ -325,15 +321,24 @@
                     axis=0,
                 )
                 high, low = split(rows)
-                waves = dot(ix_ref[...], jnp.concatenate([high, high, low], axis=0))
+                waves = dot(x_back, jnp.concatenate([high, high, low], axis=0))
                 window = pl.ds(o * groups + source, slabs, stride=groups * ch)
                 out_ref[0, window, :] = waves[:, :LANES]
                 out_ref[1, window, :] = waves[:, LANES:]
 
-        @pl.loop(0, far)
+        finish(me)
+
+        @pl.loop(0, chunks)
+        def _(chunk):
+            for shift in range(1, far):
+                source = lax.rem(me + pens - shift * near, pens)
+                column_copy(chunk, shift, source).wait_recv()
+                for side in range(1, near):
+                    row_copy(chunk, side, source, source).start()
+
+        @pl.loop(1, far)
         def _(shift):
-            source = lax.rem(me + pens - shift * near, pens)
-            finish(source)
+            finish(lax.rem(me + pens - shift * near, pens))
 
         base = me - lax.rem(me, near)
         for side in range(1, near):
@@ -394,16 +399,22 @@
         ],
         axis=0,
     )
-    inverse = lax.dynamic_slice_in_dim(
-        jnp.asarray(inverse_x_table(nx, mx)), lax.axis_index("pen") * slabs, slabs, 0
-    )
     block = 2 if slabs % 2 == 0 else 1
-    nblocks = slabs // block
+    steps = slabs // block
+    together = TOGETHER if steps % TOGETHER == 0 else 1
+    bunch = together * block
+    nblocks = steps // together
     chunks = CHUNKS if mx % CHUNKS == 0 else 1
     anywhere = pl.BlockSpec(memory_space=pl.ANY)
     return pl.pallas_call(
-        functools.partial(spectrum_kernel, my=my, nsub=nsub, pens=pens, near=near),
-        grid=(nblocks,),
+        functools.partial(
+            spectrum_kernel, my=my, nsub=nsub, pens=pens, near=near,
+            modes_code=code_of(9, FIELD_MAX * math.sqrt(ny * nz)),
+            mixed_code=code_of(
+                7, all_ch * WEIGHT_MAX * math.sqrt(2.0) * FIELD_MAX * math.sqrt(nx * ny * nz)
+            ),
+        ),
+        grid=(steps,),
         in_specs=[
             pl.BlockSpec((block, ch, ny, nz), lambda i: (i, 0, 0, 0)),
             anywhere,
@@ -421,8 +432,8 @@
         ],
         scratch_shapes=[
             pltpu.VMEM((block, nz // LANES, 2 * my * ch, LANES), F32),
-            pltpu.VMEM((nblocks, pens, block, ch, 2 * LANES), WIRE),
-            pltpu.VMEM((pens, nblocks, block, ch, 2 * LANES), WIRE),
+            pltpu.VMEM((nblocks, pens, bunch, ch, 2 * LANES), WIRE),
+            pltpu.VMEM((nblocks, pens, bunch, ch, 2 * LANES), WIRE),
             pltpu.VMEM((2, nx * ch, LANES), F32),
             pltpu.VMEM((2, 2, mx * ch, LANES), F32),
             pltpu.VMEM((2, mx, all_ch, ch, LANES), BF16),
@@ -454,63 +465,121 @@
         jnp.asarray(z_high),
         jnp.asarray(z_low),
         jnp.asarray(x_table),
-        inverse,
+        jnp.asarray(inverse_x_table(nx, mx)),
     )
 
 
 def inverse_kernel(
-    h_ref, x_ref, peer_ref, mix_ref, rows_ref, cols_ref, mask_ref, bias_ref, ty_ref, tz_ref, out_ref,
-    table,
+    start_ref, h_ref, x_ref, peer_ref, mix_ref, rows_ref, cols_ref, mask_ref, bias_ref, ty_ref, tz_ref, out_ref,
+    table, shift, even, odd,
     *, nsub, groups, ysub
 ):
+    step = pl.program_id(0)
     _, ch, ny, nz = x_ref.shape
-
-    @pl.when(pl.program_id(0) == 0)
-    def _():
-        for at, part in enumerate(split(mix_ref[...])):
-            wide = dot(dot(rows_ref[...], part).astype(BF16), cols_ref[...]) * mask_ref[...]
-            table[pl.ds(at * ch * ysub, ch * ysub), :] = wide.astype(BF16)
-
     count = LANES // MZ
-    block = lax.broadcasted_iota(jnp.int32, (ch * groups, LANES), 1) // MZ
-    real, imag = h_ref[0], h_ref[1]
-
-    def rolled(rows):
-        return [rows] + [pltpu.roll(rows, MZ * at, 1) for at in range(1, count)]
-
-    reals, imags = rolled(real), rolled(imag)
-    minus = [-rows for rows in reals]
-
-    def laid(even, odd, sub):
-        result = even[-sub % count]
-        for at in range(1, count):
-            result = jnp.where(block == at, (odd if at % 2 else even)[(at - sub) % count], result)
-        return result
-
-    tops = [laid(reals, imags, sub) for sub in range(nsub)]
-    lows = [laid(imags, minus, sub) for sub in range(nsub)]
-    for pair in range(0, ch, 2):
-        sides = []
-        for o in (pair, pair + 1):
-            window = slice(o * groups, (o + 1) * groups)
-            high, low = split(jnp.concatenate([rows[window] for rows in tops + lows], axis=0))
-            sides.append(jnp.concatenate([high, high, low], axis=0))
-        waves = dot(ty_ref[...], jnp.concatenate(sides, axis=1))
-        for at, o in enumerate((pair, pair + 1)):
-            high, low = split(waves[:, at * LANES : (at + 1) * LANES])
-            spectral = dot(jnp.concatenate([high, low], axis=1), tz_ref[...])
-            out_ref[0, o] = spectral + bias_ref[0, o]
-    for at in range(0, ny, ysub):
+    rows = ch * groups
+    scale = math.sqrt(2.0 / math.pi)
+
+    def prepare():
+        core = lax.axis_index("ch")
+        for at, part in enumerate(split(mix_ref[0])):
+            wide = lax.dot_general(
+                rows_ref[...], part, (((1,), (1,)), ((), ())), preferred_element_type=F32
+            )
+            wide = dot(wide.astype(BF16), cols_ref[core]) * mask_ref[...]
+            half = cols_ref.shape[2]
+            table[:, at * half : (at + 1) * half] = wide.astype(BF16)
+        lane = lax.broadcasted_iota(jnp.int32, shift.shape[1:], 1)
+        row = lax.broadcasted_iota(jnp.int32, shift.shape[1:], 0)
+        for o in range(ch):
+            high, low = split(jnp.full(shift.shape[1:], bias_ref[0, o] * MZ**0.5, F32))
+            value = jnp.where(row == 0, high.astype(F32), low.astype(F32))
+            value = jnp.where((row < 2) & (lane % (2 * MZ) == 0), value, 0.0)
+            shift[o] = value.astype(BF16)
+
+    def layout(ref):
+        real, imag = ref[0], ref[1]
+        block = lax.broadcasted_iota(jnp.int32, (rows, LANES), 1) // MZ
+
+        def rolled(value):
+            return [value] + [pltpu.roll(value, MZ * at, 1) for at in range(1, count)]
+
+        reals, imags = rolled(real), rolled(imag)
+        minus = [-value for value in reals]
+
+        def laid(first, second, sub):
+            result = first[-sub % count]
+            for at in range(1, count):
+                source = (second if at % 2 else first)[(at - sub) % count]
+                result = jnp.where(block == at, source, result)
+            return result
+
+        tops = [laid(reals, imags, sub) for sub in range(nsub)]
+        return tops + [laid(imags, minus, sub) for sub in range(nsub)]
+
+    def along_y(pieces, o):
+        window = slice(o * groups, (o + 1) * groups)
+        high, low = split(jnp.concatenate([value[window] for value in pieces], axis=0))
+        return jnp.concatenate([high, high, low, shift[o]], axis=0)
+
+    def spectral_pair(pieces, pair):
+        sides = [along_y(pieces, pair), along_y(pieces, pair + 1)]
+        return dot(ty_ref[...], jnp.concatenate(sides, axis=1))
+
+    def spectral_one(waves, at, o, target):
+        high, low = split(waves[:, at * LANES : (at + 1) * LANES])
+        target[o] = dot(jnp.concatenate([high, low], axis=1), tz_ref[...])
+
+    def bypass(at):
         window = slice(at, at + ysub)
         cells = [ref[0, c, window, :] for ref in (x_ref, peer_ref) for c in range(ch)]
-        both = dot(table[...], jnp.concatenate(cells, axis=0))
-        bypass = both[: ch * ysub] + both[ch * ysub :]
-        inner = bypass.reshape(ch, ysub, nz) + out_ref[0, :, window, :]
+        return dot(table[...], jnp.concatenate(cells + cells, axis=0))
+
+    def activate(at, product, source):
+        window = slice(at, at + ysub)
+        half = product.reshape(ch, ysub, nz) + source[:, window, :]
         own = x_ref[0, :, window, :].astype(F32)
-        scale = math.sqrt(2.0 / math.pi)
-        cubic = inner * (scale + (0.044715 * scale) * (inner * inner))
-        half = 0.5 * inner
-        out_ref[0, :, window, :] = own + (half + half * jnp.tanh(cubic))
+        cubic = half * (2.0 * scale + (8.0 * 0.044715 * scale) * (half * half))
+        out_ref[0, :, window, :] = (half + half * jnp.tanh(cubic)) + own
+
+    @pl.when(step == 0)
+    def _():
+        prepare()
+        pieces = layout(start_ref)
+        for pair in range(0, ch, 2):
+            waves = spectral_pair(pieces, pair)
+            for at in range(2):
+                spectral_one(waves, at, pair + at, even)
+
+    def advance(source, target):
+        pieces = layout(h_ref)
+        turns = ny // ysub
+        per = max(ch // turns, 1)
+        spaced = max(turns // ch, 1)
+        queue = {}
+        queue[0] = spectral_pair(pieces, 0)
+        product = bypass(0)
+        done = 0
+        for turn in range(turns):
+            if turn % spaced == 0:
+                for _ in range(per):
+                    if done < ch:
+                        pair = done - done % 2
+                        if done % 2 == 0 and pair + 2 < ch:
+                            queue[pair + 2] = spectral_pair(pieces, pair + 2)
+                        spectral_one(queue[pair], done % 2, done, target)
+                        done += 1
+            following = bypass((turn + 1) * ysub) if turn + 1 < turns else None
+            activate(turn * ysub, product, source)
+            product = following
+
+    @pl.when(step % 2 == 0)
+    def _():
+        advance(even, odd)
+
+    @pl.when(step % 2 == 1)
+    def _():
+        advance(odd, even)
 
 
 def whole_vmem():
@@ -550,31 +619,38 @@
 
 def inverse_field(waves, features, peer, mixing, bias, my, mz):
     slabs, ch, ny, nz = features.shape
-    all_ch = mixing.shape[0]
+    all_ch = mixing.shape[1]
     nsub = LANES // mz
     groups = my // nsub
     ysub = YSUB
+    rows = ch * groups
     cos_y, sin_y = tables(ny, my)
     cos_z, sin_z = tables(nz, mz)
     y_pair = np.stack([cos_y, -sin_y]).reshape(2, groups, nsub, ny) * my**-0.5
     y_high, y_low = split_np(y_pair.transpose(3, 0, 2, 1).reshape(ny, 2 * my))
-    y_table = np.concatenate([y_high, y_low, y_high], axis=1)
-    z_high, z_low = split_np(np.concatenate([cos_z, -sin_z]) * mz**-0.5)
+    ones = np.zeros((ny, 16), y_high.dtype)
+    ones[:, :2] = 1
+    y_table = np.concatenate([y_high, y_low, y_high, ones], axis=1)
+    z_high, z_low = split_np(np.concatenate([cos_z, -sin_z]) * (0.5 * mz**-0.5))
     copies = LANES // (2 * mz)
-    blank = [np.zeros_like(z_high)] * (copies - 2)
-    z_table = np.concatenate(
-        [z_high, z_low, *blank, z_high, np.zeros_like(z_high), *blank], axis=0
-    )
-    high_rows, high_cols = ch * ysub, all_ch * ysub
+    none = np.zeros_like(z_high)
+    blank = [none] * (copies - 2)
+    z_table = np.concatenate([z_high, z_low, *blank, z_high, none, *blank], axis=0)
     spread_rows = np.repeat(np.eye(ch), ysub, axis=0).astype(ml_dtypes.bfloat16)
-    spread_cols = np.repeat(np.eye(all_ch), ysub, axis=1).astype(ml_dtypes.bfloat16)
-    mask = np.tile(np.eye(ysub), (ch, all_ch)).astype(np.float32)
-    rows = ch * groups
+    order = np.arange(all_ch)
+    spread_cols = np.stack(
+        [
+            np.repeat((order[:, None] == np.roll(order, -core * ch)[None, :]), ysub, axis=1)
+            for core in range(2)
+        ]
+    ).astype(ml_dtypes.bfloat16)
+    mask = (0.5 * np.tile(np.eye(ysub), (ch, all_ch))).astype(np.float32)
     return pl.pallas_call(
         functools.partial(inverse_kernel, nsub=nsub, groups=groups, ysub=ysub),
         grid=(slabs,),
         in_specs=[
-            pl.BlockSpec((2, rows, LANES), lambda i: (0, i, 0)),
+            pl.BlockSpec((2, rows, LANES), lambda i: (0, 0, 0)),
+            pl.BlockSpec((2, rows, LANES), lambda i: (0, jnp.minimum(i + 1, slabs - 1), 0)),
             pl.BlockSpec((1, ch, ny, nz), lambda i: (i, 0, 0, 0)),
             pl.BlockSpec((1, ch, ny, nz), lambda i: (i, 0, 0, 0)),
             whole_vmem(),
@@ -587,14 +663,20 @@
         ],
         out_specs=pl.BlockSpec((1, ch, ny, nz), lambda i: (i, 0, 0, 0)),
         out_shape=jax.ShapeDtypeStruct((slabs, ch, ny, nz), F32),
-        scratch_shapes=[pltpu.VMEM((2 * high_rows, high_cols), BF16)],
-        compiler_params=pltpu.CompilerParams(vmem_limit_bytes=60 * 2**20),
+        scratch_shapes=[
+            pltpu.VMEM((ch * ysub, 2 * all_ch * ysub), BF16),
+            pltpu.VMEM((ch, 16, LANES), BF16),
+            pltpu.VMEM((ch, ny, nz), F32),
+            pltpu.VMEM((ch, ny, nz), F32),
+        ],
+        compiler_params=pltpu.CompilerParams(vmem_limit_bytes=48 * 2**20),
         name="inverse_field",
     )(
         waves,
+        waves,
         features,
         peer,
-        mixing.T,
+        mixing,
         jnp.asarray(spread_rows),
         jnp.asarray(spread_cols),
         jnp.asarray(mask),
@@ -653,15 +735,12 @@
     mz = MZ
     my = kept // mz
     near = 2 if pens % 2 == 0 else 1
-    core = lax.axis_index("ch")
     if owned == LANES and all_ch == 2 * ch:
         waves, peer = spectrum(features, spectral_weights, my, mz, pens, near)
     else:
         peer = lax.ppermute(features, "ch", [(0, 1), (1, 0)])
         waves = spread_spectrum(features, spectral_weights, my, mz, pens)
-    mixing = bypass_weights[0]
-    mixing = jnp.where(core == 0, mixing, jnp.roll(mixing, ch, axis=0))
-    return inverse_field(waves, features, peer, mixing, bypass_bias, my, mz)
+    return inverse_field(waves, features, peer, bypass_weights, bypass_bias, my, mz)
 
 
 def solution(mesh):

time: 110 us -> 96.4 us (0.88)
  Pallas kernels: 106 us -> 93.3 us
  other arithmetic: 1.37 us -> 0 us
    pallas_call x1, Pallas kernels: 46.9 us -> 35 us  [inverse_field(): pl.pallas_call(functools.partial(inverse_kernel, nsub=nsub, groups=groups...]
    unnamed x0 -> x15, local copies, waits for them, and re-layouts: none -> 2.38 us
    transpose x1 -> x0, other arithmetic: 1.37 us -> none  [inverse_field(): return pl.pallas_call(functools.partial(inverse_kernel, nsub=nsub, groups...]
    dynamic_slice x1 -> x0, local copies, waits for them, and re-layouts: 1.28 us -> none  [spectrum(): lax.dynamic_slice_in_dim(jnp.asarray(inverse_x_table(nx, mx)), lax.axis_i...]
    pallas_call x1, Pallas kernels: 59.4 us -> 58.2 us  [spectrum(): pl.pallas_call(functools.partial(spectrum_kernel, my=my, nsub=nsub, pens=...]
where the time goes in v2:
time: 96.4 us; the launch traced here: 95.7 us
  Pallas kernels  93.3 us (97%)
  local copies, waits for them, and re-layouts  2.38 us (2%)
    pallas_call x1, Pallas kernels, spectrum(): pl.pallas_call(functools.partial(spectrum_kernel, my=my, nsub=nsub, pens=...  58.2 us
    pallas_call x1, Pallas kernels, inverse_field(): pl.pallas_call(functools.partial(inverse_kernel, nsub=nsub, groups=groups...  35 us
    unnamed x15, local copies, waits for them, and re-layouts  2.38 us

profile of v2, /device:TPU:0, one launch (start us, length us, event | category | flops | bytes accessed | tf_op | source)
XLA Modules:
  0.0 95.7 jit_solution(15078466145197641743)
XLA Ops:
  0.0 0.8 copy.15.mix_ref
  0.8 0.0 copy-start.1
  0.8 0.0 copy-start.2
  0.8 0.0 copy-start.3
  0.8 0.0 copy-start.4
  0.8 0.0 copy-start.5
  0.8 0.0 copy-start.6
  0.8 58.2 %spectrum.1 = (f32[2,2048,128]{2,1,0:T(8,128)}, bf16[16,16,128,256]{3,2,1,0:T(8,128)(2,1)}) custom-call(bf16[16,16,128,256]{3,2,1,0:T(8,128)(2,1)} %x_ref.3, bf16[16,16,128,256]{3,2,1,0:T(8,128)(2,1)} %x_ref.3, bf16[1,2,16,32,16,128]{5,4,3,2,1,0:T(8,128)(2,1)} %weight_ref.1, bf16[128,128]{1,0:T(8,128)(2,1)} %constant.20.clone.ty_ref, ...), custom_call_target="tpu_custom_call" | custom-call | flops 8589934592 | bytes 67108864 | tf_op jit(solution)/shard_map/spectrum/pallas_call | solution.py:409
  59.1 0.0 copy-done.1
  59.1 0.0 copy-done.2
  59.1 0.0 copy-done.3
  59.1 0.0 copy-done.4
  59.1 0.0 copy-done.5
  59.1 0.0 copy-done.6
  59.1 0.0 copy-start
  59.1 1.6 %copy-done = f32[2,2048,128]{2,1,0:T(8,128)S(1)} copy-done((f32[2,2048,128]{2,1,0:T(8,128)S(1)}, f32[2,2048,128]{2,1,0:T(8,128)}, u32[]{:S(2)}) %copy-start) | copy-done | bytes 2097176
  60.7 35.0 %inverse_field.1 = f32[16,16,128,256]{3,2,1,0:T(8,128)} custom-call(f32[2,2048,128]{2,1,0:T(8,128)S(1)} %copy-done, f32[2,2048,128]{2,1,0:T(8,128)S(1)} %copy-done, bf16[16,16,128,256]{3,2,1,0:T(8,128)(2,1)} %x_ref.3, bf16[16,16,128,256]{3,2,1,0:T(8,128)(2,1)} %get-tuple-element.8.peer_ref, f32[1,32,16]{2,1,0:T(8,128)S(1)} %copy.15.mix_ref, ...), custom_call_target="tpu_custom_call" | custom-call | tf_op jit(solution)/shard_map/inverse_field/pallas_call | solution.py:648
Async XLA Ops:
  0.8 58.3 %copy-start.1 = (bf16[256,256]{1,0:T(8,128)(2,1)S(1)}, bf16[256,256]{1,0:T(8,128)(2,1)}, u32[]{:S(2)}) copy-start(bf16[256,256]{1,0:T(8,128)(2,1)} %constant.29.clone.tz_ref) | copy-start | bytes 393220
  0.8 58.3 %copy-start.2 = (f32[128,256]{1,0:T(8,128)S(1)}, f32[128,256]{1,0:T(8,128)}, u32[]{:S(2)}) copy-start(f32[128,256]{1,0:T(8,128)} %constant.27.clone.mask_ref) | copy-start | bytes 393220
  0.8 58.3 %copy-start.3 = (bf16[128,208]{1,0:T(8,128)(2,1)S(1)}, bf16[128,208]{1,0:T(8,128)(2,1)}, u32[]{:S(2)}) copy-start(bf16[128,208]{1,0:T(8,128)(2,1)} %constant.28.clone.ty_ref) | copy-start | bytes 159748
  0.8 58.3 %copy-start.4 = (bf16[2,32,256]{2,1,0:T(8,128)(2,1)S(1)}, bf16[2,32,256]{2,1,0:T(8,128)(2,1)}, u32[]{:S(2)}) copy-start(bf16[2,32,256]{2,1,0:T(8,128)(2,1)} %constant.26.clone.cols_ref) | copy-start | bytes 98308
  0.8 58.3 %copy-start.5 = (bf16[128,16]{1,0:T(8,128)(2,1)S(1)}, bf16[128,16]{1,0:T(8,128)(2,1)}, u32[]{:S(2)}) copy-start(bf16[128,16]{1,0:T(8,128)(2,1)} %constant.25.clone.rows_ref) | copy-start | bytes 12292
  0.8 58.3 %copy-start.6 = (f32[1,16]{1,0:T(1,128)S(1)}, f32[1,16]{1,0:T(1,128)}, u32[]{:S(2)}) copy-start(f32[1,16]{1,0:T(1,128)} %bias_ref.1) | copy-start | bytes 196
  59.1 1.6 %copy-start = (f32[2,2048,128]{2,1,0:T(8,128)S(1)}, f32[2,2048,128]{2,1,0:T(8,128)}, u32[]{:S(2)}) copy-start(f32[2,2048,128]{2,1,0:T(8,128)} %get-tuple-element.7.start_ref.h_ref) | copy-start | bytes 6291460

commit v3 on v2

--- a/solution.py
+++ b/solution.py
@@ -77,8 +77,8 @@
 
 
 MESH = pl.DeviceIdType.MESH
-CHUNKS = 4
-TOGETHER = 2
+CHUNKS = 2
+TOGETHER = 1
 
 
 def odd_power(value, power):
@@ -110,8 +110,8 @@
 
 def spectrum_kernel(
     x_ref, feat_ref, weight_ref, ty_ref, bh_ref, bl_ref, tx_ref, ix_ref, out_ref, field_ref,
-    y_ref, send, recv, wide, fx, weight, partial, every, plain,
-    send_sem, recv_sem, gsend_sem, grecv_sem, psend_sem, fsend_sem, frecv_sem, xsem, wsem,
+    tables_ref, y_ref, send, recv, wide, fx, weight, partial, every, plain,
+    send_sem, recv_sem, gsend_sem, grecv_sem, psend_sem, fsend_sem, frecv_sem, xsem, wsem, tsem,
     *, my, nsub, pens, near, modes_code, mixed_code,
 ):
     step = pl.program_id(0)
@@ -121,7 +121,6 @@
     block, ch, _, nz = x_ref.shape
     parts = nz // LANES
     groups = my // nsub
-    half = my * ch
     mx = every.shape[1]
     far = pens // near
     nx = wide.shape[1] // ch
@@ -182,6 +181,10 @@
     def weight_copy():
         return pltpu.make_async_copy(weight_ref.at[0], weight, wsem)
 
+    def table_copy(at):
+        source = (bh_ref, bl_ref)[at]
+        return pltpu.make_async_copy(source, tables_ref.at[at], tsem.at[at])
+
     def pair_copy():
         return pltpu.make_async_remote_copy(
             src_ref=fx.at[0],
@@ -194,42 +197,60 @@
 
     @pl.when(step == 0)
     def _():
+        for at in range(2):
+            table_copy(at).start()
         barrier = pltpu.get_barrier_semaphore()
         for shift in range(1, pens):
             pl.semaphore_signal(
                 barrier, inc=1, device_id={"pen": lax.rem(me + shift, pens)}, device_id_type=MESH
             )
         pl.semaphore_signal(barrier, inc=1, device_id={"ch": 1 - core}, device_id_type=MESH)
-        pl.semaphore_wait(barrier, pens)
-        for at in range(nblocks):
-            field_copy(at).start()
         weight_copy().start()
 
+    tall = ty_ref.shape[0] // 2
+    top = my // 2
     for b in range(block):
         for c in range(ch):
             both = dot(ty_ref[...], x_ref[b, c])
-            rows = both[: 2 * my] + both[2 * my :]
+            rows = both[:tall] + both[tall:]
             for part in range(parts):
-                y_ref[b, part, pl.ds(c, 2 * my, stride=ch), :] = rows[
+                y_ref[b, part, pl.ds(c, tall, stride=ch), :] = rows[
                     :, part * LANES : (part + 1) * LANES
                 ]
+
+    def wave(b, part, sine, index):
+        freq = index if index < top else my - index
+        if sine and freq == 0:
+            return jnp.zeros((ch, LANES), F32)
+        row = (top + freq if sine else freq) * ch
+        value = y_ref[b, part, row : row + ch, :]
+        return -value if sine and index >= top else value
+
     highs, lows = [], []
     for b in range(block):
-        pieces = []
-        for cs in range(2):
-            loaded = [
-                y_ref[b, part, cs * half : (cs + 1) * half, :].reshape(groups, nsub, ch, LANES)
-                for part in range(parts)
-            ]
-            for sub in range(nsub):
-                for part in range(parts):
-                    pieces.append(loaded[part][:, sub].reshape(groups * ch, LANES))
+        pieces = [
+            jnp.concatenate(
+                [wave(b, part, sine, group * nsub + sub) for group in range(groups)], axis=0
+            )
+            for sine in range(2)
+            for sub in range(nsub)
+            for part in range(parts)
+        ]
         high, low = split(jnp.concatenate(pieces, axis=1))
         highs.append(high)
         lows.append(low)
     high = jnp.concatenate(highs, axis=0)
     low = jnp.concatenate(lows, axis=0)
-    result = dot(high, bh_ref[...]) + dot(low, bh_ref[...]) + dot(high, bl_ref[...])
+
+    @pl.when(step == 0)
+    def _():
+        pl.semaphore_wait(pltpu.get_barrier_semaphore(), pens)
+        for at in range(nblocks):
+            field_copy(at).start()
+        for at in range(2):
+            table_copy(at).wait()
+
+    result = dot(high, tables_ref[0]) + dot(low, tables_ref[0]) + dot(high, tables_ref[1])
     result = encode(result, *modes_code).reshape(block, groups, ch, 2 * LANES)
     group, turn = step // together, step % together
     for b in range(block):
@@ -389,7 +410,13 @@
     nx = slabs * pens
     nsub = LANES // mz
     groups = my // nsub
-    y_table, z_high, z_low = forward_tables(ny, nz, my, mz)
+    _, z_high, z_low = forward_tables(ny, nz, my, mz)
+    top = my // 2
+    angles = (np.arange(top + 1)[:, None] * np.arange(ny)[None, :]) % ny * (2.0 * math.pi / ny)
+    tall = -(-(my + 1) // 8) * 8
+    y_rows = np.zeros((tall, ny))
+    y_rows[: my + 1] = np.concatenate([np.cos(angles), np.sin(angles[1:])]) * ny**-0.5
+    y_table = np.concatenate(split_np(y_rows), axis=0)
     cos_x, sin_x = tables(nx, mx)
     x_high, x_low = split_np(np.concatenate([cos_x, sin_x]) * nx**-0.5)
     x_table = np.concatenate(
@@ -405,7 +432,7 @@
     bunch = together * block
     nblocks = steps // together
     chunks = CHUNKS if mx % CHUNKS == 0 else 1
-    anywhere = pl.BlockSpec(memory_space=pl.ANY)
+    anywhere = pl.BlockSpec(memory_space=pltpu.HBM)
     return pl.pallas_call(
         functools.partial(
             spectrum_kernel, my=my, nsub=nsub, pens=pens, near=near,
@@ -420,8 +447,8 @@
             anywhere,
             anywhere,
             whole_vmem(),
-            whole_vmem(),
-            whole_vmem(),
+            anywhere,
+            anywhere,
             whole_vmem(),
             whole_vmem(),
         ],
@@ -431,7 +458,8 @@
             jax.ShapeDtypeStruct(features.shape, features.dtype),
         ],
         scratch_shapes=[
-            pltpu.VMEM((block, nz // LANES, 2 * my * ch, LANES), F32),
+            pltpu.VMEM((2, *z_high.shape), BF16),
+            pltpu.VMEM((block, nz // LANES, tall * ch, LANES), F32),
             pltpu.VMEM((nblocks, pens, bunch, ch, 2 * LANES), WIRE),
             pltpu.VMEM((nblocks, pens, bunch, ch, 2 * LANES), WIRE),
             pltpu.VMEM((2, nx * ch, LANES), F32),
@@ -449,9 +477,10 @@
             pltpu.SemaphoreType.DMA((nblocks,)),
             pltpu.SemaphoreType.DMA((2,)),
             pltpu.SemaphoreType.DMA,
+            pltpu.SemaphoreType.DMA((2,)),
         ],
         compiler_params=pltpu.CompilerParams(
-            vmem_limit_bytes=60 * 2**20, collective_id=0, has_side_effects=True
+            vmem_limit_bytes=64900000, collective_id=0, has_side_effects=True
         ),
         cost_estimate=pl.CostEstimate(
             flops=32 * slabs * ch * my * ny * nz, bytes_accessed=8 * features.size, transcendentals=0
@@ -669,7 +698,7 @@
             pltpu.VMEM((ch, ny, nz), F32),
             pltpu.VMEM((ch, ny, nz), F32),
         ],
-        compiler_params=pltpu.CompilerParams(vmem_limit_bytes=48 * 2**20),
+        compiler_params=pltpu.CompilerParams(vmem_limit_bytes=60 * 2**20),
         name="inverse_field",
     )(
         waves,

time: 96.4 us -> 93.1 us (0.966)
  Pallas kernels: 93.3 us -> 91 us
  local copies, waits for them, and re-layouts: 2.38 us -> 1.36 us
    pallas_call x1, Pallas kernels: 58.2 us -> 55.5 us  [spectrum(): pl.pallas_call(functools.partial(spectrum_kernel, my=my, nsub=nsub, pens=...]
    unnamed x15 -> x1, local copies, waits for them, and re-layouts: 2.38 us -> 1.36 us
where the time goes in v3:
time: 93.1 us; the launch traced here: 92.4 us
  Pallas kernels  91 us (98%)
  local copies, waits for them, and re-layouts  1.36 us (1%)
    pallas_call x1, Pallas kernels, spectrum(): pl.pallas_call(functools.partial(spectrum_kernel, my=my, nsub=nsub, pens=...  55.5 us
    pallas_call x1, Pallas kernels, inverse_field(): pl.pallas_call(functools.partial(inverse_kernel, nsub=nsub, groups=groups...  35.6 us

profile of v3, /device:TPU:0, one launch (start us, length us, event | category | flops | bytes accessed | tf_op | source)
XLA Modules:
  0.0 92.4 jit_solution(263221228027119373)
XLA Ops:
  0.0 1.4 %copy.15.mix_ref = f32[1,32,16]{2,1,0:T(8,128)} copy(f32[1,32,16]{1,2,0:T(8,128)} %param.16) | data formatting | bytes 4096 | tf_op args[2]
  1.4 55.5 %spectrum.1 = (f32[2,2048,128]{2,1,0:T(8,128)}, bf16[16,16,128,256]{3,2,1,0:T(8,128)(2,1)}) custom-call(bf16[16,16,128,256]{3,2,1,0:T(8,128)(2,1)} %x_ref.3, bf16[16,16,128,256]{3,2,1,0:T(8,128)(2,1)} %x_ref.3, bf16[1,2,16,32,16,128]{5,4,3,2,1,0:T(8,128)(2,1)} %weight_ref.1, bf16[80,128]{1,0:T(8,128)(2,1)} %constant.20.clone.ty_ref, ...), custom_call_target="tpu_custom_call" | custom-call | flops 8589934592 | bytes 67108864 | tf_op jit(solution)/shard_map/spectrum/pallas_call | solution.py:436
  56.8 35.6 %inverse_field.1 = f32[16,16,128,256]{3,2,1,0:T(8,128)} custom-call(f32[2,2048,128]{2,1,0:T(8,128)} %get-tuple-element.7.start_ref.h_ref, f32[2,2048,128]{2,1,0:T(8,128)} %get-tuple-element.7.start_ref.h_ref, bf16[16,16,128,256]{3,2,1,0:T(8,128)(2,1)} %x_ref.3, bf16[16,16,128,256]{3,2,1,0:T(8,128)(2,1)} %get-tuple-element.8.peer_ref, ...), custom_call_target="tpu_custom_call" | custom-call | tf_op jit(solution)/shard_map/inverse_field/pallas_call | solution.py:677
